TPU v7x, 32 devices: a whole 2x2x4 slice. The times are simulated.
32 devices in a mesh: freq: 4 (over y, core), ga: 8 (over z, x).
Axes of the slice: x: 2, y: 2, z: 4, core: 2. Of those that a mesh axis runs over, the one named last changes fastest.
Arguments:
- screened: bfloat16 [24, 8192, 8192], P('freq', None, 'ga'), may hold values from -0.0625 to 0.0625
- elements: bfloat16 [512, 8192], P(None, 'ga'), may hold values from -6 to 6
- energies: float32 [512], replicated, may hold values from -3 to 3
- occupied: int32 [512], replicated, may hold values 0 or 1
- nodes: float32 [24], replicated, may hold values from 0.1 to 10
- quad_weights: float32 [24], replicated, may hold values from 0.05 to 1
- slot_freq: int32 [24], P('freq'), may hold values from 0 to 23, each once
Outputs:
- sigma: float32 [512, 512], P('ga')
All inputs are finite; a program needn't handle non-finite values.
Results may differ from a plain program's by a relative error of at most 0.0042.
Values may be sent and summed in bfloat16 or wider, within the bound.
No kernel may reach another device: no remote copies, remote signals or barrier semaphores. Data moves between devices by JAX's collectives and lax.ppermute only.
A program may use at most 192 MiB of HBM per device.

v0:
```python
import math
import jax
import jax.numpy as jnp
from jax import lax
from jax.sharding import PartitionSpec as P

NG = 8192
SCISSOR = 0.5


def body(screened, elements, energies, occupied, nodes, quad_weights, slot_freq):
    picks = (slot_freq[:, None] == jnp.arange(nodes.shape[0], dtype=jnp.int32)[None, :]).astype(
        jnp.float32
    )
    node = jnp.dot(picks, nodes, precision=lax.Precision.HIGHEST)
    weight = jnp.dot(picks, quad_weights, precision=lax.Precision.HIGHEST)
    shift = energies + SCISSOR * (1.0 - 2.0 * occupied.astype(jnp.float32))
    coeff = (
        weight[:, None]
        * shift[None, :]
        / (shift[None, :] * shift[None, :] + node[:, None] * node[:, None])
    )
    rows = screened
    proj = jnp.einsum(
        "nk,fkc->fnc",
        lax.all_gather(elements, "ga", axis=1, tiled=True),
        rows,
        preferred_element_type=jnp.float32,
    )
    weighted = jnp.sum(coeff[:, :, None] * proj, axis=0).astype(jnp.bfloat16)
    partial_value = lax.dot_general(
        weighted, elements, (((1,), (1,)), ((), ())), preferred_element_type=jnp.float32
    )
    rows = lax.psum_scatter(partial_value, "ga", scatter_dimension=0, tiled=True)
    block = lax.psum(rows, "freq")
    return block / math.sqrt(NG)


def solution(mesh):
    return jax.shard_map(
        body,
        mesh=mesh,
        in_specs=(P("freq", None, "ga"), P(None, "ga"), P(), P(), P(), P(), P("freq")),
        out_specs=P("ga", None),
        check_vma=False,
    )
```

profile of v0, /device:TPU:0, one launch (start us, length us, event | category | flops | bytes accessed | tf_op | source)
XLA Modules:
  0.0 303.2 jit_solution(17331923169905364043)
XLA Ops:
  6.5 0.0 copy-start
  6.5 0.0 all-gather.2.cloned.1.call-start
  6.5 0.7 all-gather.2.cloned.1.call-update
  7.3 0.0 reduce-scatter.2.cloned.1.call-start
  7.3 0.0 copy-done
  7.3 0.8 convolution_bitcast_fusion.1
  8.2 0.9 fusion.4
  9.0 0.7 fusion.11
  9.7 0.1 add_divide_fusion
  9.8 0.0 copy-start.1
  9.8 126.9 %all-gather.2.cloned.1.call-done = bf16[512,8192]{1,0:T(8,128)(2,1)} async-done(((bf16[512,1024]{1,0:T(8,128)(2,1)}), bf16[512,8192]{1,0:T(8,128)(2,1)}) %all-gather.2.cloned.1.call-update) | async-done | bytes 8388624 | tf_op jit(solution)/shard_map/all_gather | solution.py:26
  136.7 61.0 %multiply_reduce_fusion = bf16[1024,512]{1,0:T(8,128)(2,1)S(1)} fusion(f32[6,512]{1,0:T(8,128)S(1)} %add_divide_fusion, bf16[6,8192,1024]{2,1,0:T(8,128)(2,1)} %param.7, bf16[512,8192]{1,0:T(8,128)(2,1)} %all-gather.2.cloned.1.call-done), kind=kOutput, calls=%fused_computation | convolution fusion | flops 51545374720 | bytes 110112768 | tf_op jit(solution)/shard_map/nk,fkc->fnc/dot_general | solution.py:24
  197.7 0.0 copy-done.1
  197.7 1.7 fusion.12
  199.4 0.0 reduce-scatter.2.cloned.1.call-update
  199.5 0.0 all-reduce.2.cloned.1.call-start
  199.5 62.5 %reduce-scatter.2.cloned.1.call-done = f32[64,512]{1,0:T(8,128)} async-done(((f32[512,512]{1,0:T(8,128)}), f32[64,512]{1,0:T(8,128)}) %reduce-scatter.2.cloned.1.call-update) | async-done | bytes 131088 | tf_op jit(solution)/shard_map/reduce_scatter | solution.py:34
  262.0 0.0 all-reduce.2.cloned.1.call-update
  262.0 33.1 %all-reduce.2.cloned.1.call-done = f32[64,512]{1,0:T(8,128)} async-done(((f32[64,512]{1,0:T(8,128)}), f32[64,512]{1,0:T(8,128)}) %all-reduce.2.cloned.1.call-update) | async-done | bytes 131088 | tf_op jit(solution)/shard_map/psum | solution.py:35
  295.1 1.6 broadcast_multiply_fusion
Async XLA Ops:
  6.5 0.8 copy-start
  6.5 130.2 %all-gather.2.cloned.1.call-start = ((), (), s32[]{:S(2)}) async-start(), calls=%async_computation.1 | async-start | bytes 9437184 | tf_op jit(solution)/shard_map/all_gather | solution.py:26
  7.3 254.7 %reduce-scatter.2.cloned.1.call-start = ((), (), s32[]{:S(2)}) async-start(), calls=%async_computation.2 | async-start | bytes 1179648 | tf_op jit(solution)/shard_map/reduce_scatter | solution.py:34
  9.8 187.9 %copy-start.1 = (bf16[512,1024]{1,0:T(8,128)(2,1)S(1)}, bf16[512,1024]{1,0:T(8,128)(2,1)}, u32[]{:S(2)}) copy-start(bf16[512,1024]{1,0:T(8,128)(2,1)} %param.8) | copy-start | bytes 3145732
  199.5 95.7 %all-reduce.2.cloned.1.call-start = ((), (), s32[]{:S(2)}) async-start(), calls=%async_computation.3 | async-start | bytes 262144 | tf_op jit(solution)/shard_map/psum | solution.py:35
Sparse Core Ops, SparseCore 0:
  9.5 127.1 all-gather.1
  199.6 62.3 reduce-scatter.1
  264.3 30.7 all-reduce.1
where the time goes:
time: 303 us
  waiting for transfers between devices  223 us (74%)
  matrix products  64.4 us (21%)
  between operations  13.1 us (4%)
    all_gather x1, waiting for transfers between devices, body(): lax.all_gather(elements, 'ga', axis=1, tiled=True)  127 us
    reduce_scatter x1, waiting for transfers between devices, body(): lax.psum_scatter(partial_value, 'ga', scatter_dimension=0, tiled=True)  62.5 us
    dot_general x1, matrix products, body(): jnp.einsum('nk,fkc->fnc', lax.all_gather(elements, 'ga', axis=1, tiled=Tr...  61 us
    psum x1, waiting for transfers between devices, body(): block = lax.psum(rows, 'freq')  33.1 us
  transfers between devices with their start and end apart: 3, of which 3 were waited for; matrix products, arithmetic and copies ran while one was open for 1% of the time, Pallas kernels for 0%

commit v1 on v0

--- a/solution.py
+++ b/solution.py
@@ -32,7 +32,7 @@
         weighted, elements, (((1,), (1,)), ((), ())), preferred_element_type=jnp.float32
     )
     rows = lax.psum_scatter(partial_value, "ga", scatter_dimension=0, tiled=True)
-    block = lax.psum(rows, "freq")
+    block = jnp.sum(lax.all_gather(rows, "freq"), axis=0)
     return block / math.sqrt(NG)
 
 

time: 303 us -> 277 us (0.914)
  waiting for transfers between devices: 223 us -> 190 us
  blocking collectives: 0 us -> 7.33 us
    psum x1 -> x0, waiting for transfers between devices: 33.1 us -> none  [body(): block = lax.psum(rows, 'freq')]
    all_gather x0 -> x1, blocking collectives: none -> 7.33 us  [body(): block = jnp.sum(lax.all_gather(rows, 'freq'), axis=0)]
  transfers between devices with their start and end apart: 3 -> 2, of which waited for: 3 -> 2; matrix products, arithmetic and copies ran while one was open for 1% -> 1% of each run, Pallas kernels for 0% -> 0%
where the time goes in v1:
time: 277 us
  waiting for transfers between devices  190 us (69%)
  matrix products  64.4 us (23%)
  between operations  13.4 us (5%)
  blocking collectives  7.33 us (3%)
    all_gather x1, waiting for transfers between devices, body(): lax.all_gather(elements, 'ga', axis=1, tiled=True)  127 us
    reduce_scatter x1, waiting for transfers between devices, body(): lax.psum_scatter(partial_value, 'ga', scatter_dimension=0, tiled=True)  62.5 us
    dot_general x1, matrix products, body(): jnp.einsum('nk,fkc->fnc', lax.all_gather(elements, 'ga', axis=1, tiled=Tr...  61 us
    all_gather x1, blocking collectives, body(): block = jnp.sum(lax.all_gather(rows, 'freq'), axis=0)  7.33 us
  transfers between devices with their start and end apart: 2, of which 2 were waited for; matrix products, arithmetic and copies ran while one was open for 1% of the time, Pallas kernels for 0%

profile of v1, /device:TPU:0, one launch (start us, length us, event | category | flops | bytes accessed | tf_op | source)
XLA Modules:
  0.0 276.9 jit_solution(7691311006156911251)
XLA Ops:
  6.5 0.0 copy-start
  6.5 0.0 all-gather.3.cloned.1.call-start
  6.5 0.7 all-gather.3.cloned.1.call-update
  7.3 0.0 reduce-scatter.2.cloned.1.call-start
  7.3 0.0 copy-done
  7.3 0.8 convolution_bitcast_fusion.1
  8.2 0.9 fusion.4
  9.0 0.7 fusion.11
  9.7 0.1 add_divide_fusion
  9.8 0.0 copy-start.1
  9.8 126.9 %all-gather.3.cloned.1.call-done = bf16[512,8192]{1,0:T(8,128)(2,1)} async-done(((bf16[512,1024]{1,0:T(8,128)(2,1)}), bf16[512,8192]{1,0:T(8,128)(2,1)}) %all-gather.3.cloned.1.call-update) | async-done | bytes 8388624 | tf_op jit(solution)/shard_map/all_gather | solution.py:26
  136.7 61.0 %multiply_reduce_fusion = bf16[1024,512]{1,0:T(8,128)(2,1)S(1)} fusion(f32[6,512]{1,0:T(8,128)S(1)} %add_divide_fusion, bf16[6,8192,1024]{2,1,0:T(8,128)(2,1)} %param.7, bf16[512,8192]{1,0:T(8,128)(2,1)} %all-gather.3.cloned.1.call-done), kind=kOutput, calls=%fused_computation | convolution fusion | flops 51545374720 | bytes 110112768 | tf_op jit(solution)/shard_map/nk,fkc->fnc/dot_general | solution.py:24
  197.7 0.0 copy-done.1
  197.7 1.7 fusion.12
  199.5 0.0 reduce-scatter.2.cloned.1.call-update
  199.5 62.5 %reduce-scatter.2.cloned.1.call-done = f32[64,512]{1,0:T(8,128)} async-done(((f32[512,512]{1,0:T(8,128)}), f32[64,512]{1,0:T(8,128)}) %reduce-scatter.2.cloned.1.call-update) | async-done | bytes 131088 | tf_op jit(solution)/shard_map/reduce_scatter | solution.py:34
  262.0 7.3 %all-gather = f32[256,512]{1,0:T(8,128)S(1)} all-gather(f32[64,512]{1,0:T(8,128)} %reduce-scatter.2.cloned.1.call-done), channel_id=2, replica_groups=mesh['freq'=4,'ga'=8] {'freq'}, dimensions={0}, use_global_device_ids=true | all-gather | bytes 655360 | tf_op jit(solution)/shard_map/all_gather | solution.py:35
  269.4 0.7 broadcast_multiply_fusion
  (1 shorter events, 0.0 us)
Async XLA Ops:
  6.5 0.8 copy-start
  6.5 130.2 %all-gather.3.cloned.1.call-start = ((), (), s32[]{:S(2)}) async-start(), calls=%async_computation.1 | async-start | bytes 9437184 | tf_op jit(solution)/shard_map/all_gather | solution.py:26
  7.3 254.7 %reduce-scatter.2.cloned.1.call-start = ((), (), s32[]{:S(2)}) async-start(), calls=%async_computation.2 | async-start | bytes 1179648 | tf_op jit(solution)/shard_map/reduce_scatter | solution.py:34
  9.8 187.9 %copy-start.1 = (bf16[512,1024]{1,0:T(8,128)(2,1)S(1)}, bf16[512,1024]{1,0:T(8,128)(2,1)}, u32[]{:S(2)}) copy-start(bf16[512,1024]{1,0:T(8,128)(2,1)} %param.8) | copy-start | bytes 3145732
Sparse Core Ops, SparseCore 0:
  9.5 127.1 all-gather.2
  199.6 62.3 reduce-scatter.1
